TPU v7x, 32 devices: a whole 2x2x4 slice. The times are simulated.
32 devices in a mesh: gx: 4 (over x, core), gy: 2 (over y), gz: 4 (over z).
Axes of the slice: x: 2, y: 2, z: 4, core: 2. Of those that a mesh axis runs over, the one named last changes fastest.
Arguments:
- grid_inputs: bfloat16 [186, 256, 256], P(None, 'gx', 'gy'), may hold values from -6 to 6
- embed_w1: bfloat16 [512, 186], replicated, may hold values from -0.4375 to 0.4375
- embed_b1: float32 [512], replicated, may hold values from -3 to 3
- embed_w2: bfloat16 [512, 512], replicated, may hold values from -0.25 to 0.25
- embed_gain: float32 [512], replicated, may hold values from 0.1 to 1.9
- edge_w1: bfloat16 [512, 1536], replicated, may hold values from -0.15625 to 0.15625
- edge_b1: float32 [512], replicated, may hold values from -3 to 3
- edge_w2: bfloat16 [512, 512], replicated, may hold values from -0.25 to 0.25
- message_gain: float32 [512], replicated, may hold values from 0.1 to 1.9
- message_bias: float32 [512], replicated, may hold values from -3 to 3
- mesh_latent: bfloat16 [512, 4, 2, 256], P('gz', 'gx', 'gy'), may hold values from -6 to 6
- edge_latent: bfloat16 [512, 4, 2, 2048], P('gz', 'gx', 'gy'), may hold values from -6 to 6
- senders: int32 [4, 2, 2048], P('gx', 'gy'), may hold values from 0 to 65535, as said below
- receivers: int32 [4, 2, 2048], P('gx', 'gy'), may hold values from 0 to 2047, as said below
- edge_counts: int32 [4, 2], P('gx', 'gy'), may hold values from 1 to 2048, as said below
Outputs:
- mesh_out: bfloat16 [512, 4, 2, 256], P('gz', 'gx', 'gy')
- grid_latent: bfloat16 [512, 256, 256], P('gz', 'gx', 'gy')
Inputs may be any that keep to these rules, and one draw needn't show every extreme that they name: `senders`: an edge of tile (b, c) has its sender's row within 8 rows of rows b * 64 to (b + 1) * 64 - 1, clipped to the grid, and its column within 8 columns, cyclically, of columns c * 128 to (c + 1) * 128 - 1; this holds in every slot. `receivers`: an edge of tile t is received by a node of that tile, t * 256 to (t + 1) * 256 - 1, in every slot. `edge_counts`: the live edges of a tile are its first slots; some tile holds 2048 live edges.
All inputs are finite; a program needn't handle non-finite values.
Results may differ from a plain program's by a relative error of at most 0.0049.
Values may be sent and summed in bfloat16 or wider, within the bound.
A program may use at most 128 MiB of HBM per device.

v0:
```python
import jax
import jax.numpy as jnp
from jax import lax
from jax.experimental import pallas as pl
from jax.experimental.pallas import tpu as pltpu
from jax.sharding import PartitionSpec as P

HALO = 8
ROWS = 16
GROUP = 4

epsilon = 1e-05
F32 = jnp.float32
BF16 = jnp.bfloat16


def half_silu(half):
    return half + half * jnp.tanh(half)


def centre(values):
    average = jnp.mean(values, axis=0, keepdims=True)
    centred = values - average
    spread = jnp.mean(centred * centred, axis=0, keepdims=True)
    return average, lax.rsqrt(spread + epsilon)


def onehot_of(index_row, first, count):
    ids = lax.broadcasted_iota(jnp.int32, (count, index_row.shape[1]), 0)
    return jnp.where(ids == index_row - first, 1.0, 0.0).astype(BF16)


MESH = pl.DeviceIdType.MESH


def partner(dx, dy, dz):
    ids = {}
    for axis, step in (("gx", dx), ("gy", dy), ("gz", dz)):
        size = lax.axis_size(axis)
        ids[axis] = lax.rem(lax.axis_index(axis) + (step + size), size)
    return ids


def split(values, size):
    if size & (size - 1) == 0:
        return lax.shift_right_logical(values, size.bit_length() - 1), values & (size - 1)
    return values // size, values % size


def locate(send, receive, live, near_ref, send_ref, nodes, lat, lon):
    band = lax.axis_index("gx")
    sector = lax.axis_index("gy")
    lon_total = lon * lax.axis_size("gy")
    slot_ids = lax.broadcasted_iota(jnp.int32, receive.shape, 1)
    tile = band * lax.axis_size("gy") + sector
    near_ref[...] = jnp.where(slot_ids < live, receive - tile * nodes, -1)
    row, column = split(send, lon_total)
    row = row - band * lat
    column = split(column - sector * lon + (HALO + lon_total), lon_total)[1] - HALO
    above, below = row < 0, row >= lat
    west, east = column < 0, column >= lon
    outside_row = jnp.where(above, 1, jnp.where(below, 1, 0))
    outside_column = jnp.where(west, 1, jnp.where(east, 1, 0))
    send_ref[0:1, :] = jnp.where(outside_row + outside_column == 0, row * lon + column, -1)
    strip = HALO * lon
    tall = lat * HALO
    row_index = jnp.where(above, row + HALO, row - lat + HALO) * lon + column
    beside = jnp.where(west, column + HALO, column - lon)
    column_index = 2 * strip + jnp.where(west, 0, tall) + row * HALO + beside
    corner = jnp.where(above, 0, 2) + jnp.where(west, 0, 1)
    corner_row = jnp.where(above, row + ROWS, row - lat)
    corner_index = 2 * (strip + tall) + (corner * ROWS + corner_row) * HALO + beside
    send_ref[1:2, :] = jnp.where(
        outside_column == 0,
        jnp.where(outside_row == 0, -1, row_index),
        jnp.where(outside_row == 0, column_index, corner_index),
    )


def kernel(
    x_hbm, w1_ref, w2_ref, e1_hbm, e2_hbm, b1_ref, gain_ref, eb1_ref, mgain_ref, mbias_ref,
    mesh_ref, edge_ref, senders_ref, receivers_ref, count_ref,
    out_hbm, mean_ref,
    x_ref, wide, w1, cols, e1_ref, e2_ref, w1_wide, vec_ref, near_ref, send_ref, gathered, pre_ref, out_wide, stage,
    rows_send, cols_send, rows_recv, cols_recv, corner_recv,
    assigned, nodes_all, totals, parts,
    x_sem, out_sem, w_sem, halo_send, halo_recv, z_send, z_recv,
):
    tiles, channels, rows, lon = x_ref.shape
    padded = w1.shape[1]
    latent, share = assigned.shape
    shard, nodes = mesh_ref.shape
    slots = edge_ref.shape[1]
    layers = slots // share
    me = lax.axis_index("gz")
    mine = pl.ds(pl.multiple_of(me * shard, shard), shard)

    diagonals = ((1, 1), (1, -1), (-1, 1), (-1, -1))
    around = [(1, 0, 0), (-1, 0, 0), (0, 1, 0), (0, -1, 0)]
    around += [(dx, dy, 0) for dx, dy in diagonals]
    around += [(0, 0, k) for k in range(1, layers)]
    barrier = pltpu.get_barrier_semaphore()
    for offset in around:
        pl.semaphore_signal(barrier, inc=1, device_id=partner(*offset), device_id_type=MESH)
    loads = [
        pltpu.make_async_copy(x_hbm.at[:, pl.ds(t * rows, rows), :], x_ref.at[t], x_sem.at[t])
        for t in range(tiles)
    ]
    weights = [
        pltpu.make_async_copy(e1_hbm, e1_ref, w_sem.at[0]),
        pltpu.make_async_copy(e2_hbm, e2_ref, w_sem.at[1]),
    ]
    for load in loads + weights:
        load.start()

    w1_wide[...] = jnp.zeros_like(w1_wide)
    w1_wide[:channels, :] = w1_ref[...].astype(F32) * 0.5
    w1[...] = w1_wide[...].T[:, :padded].astype(BF16)
    vec_ref[...] = jnp.zeros_like(vec_ref)
    for i, ref in enumerate((b1_ref, gain_ref, eb1_ref, mgain_ref, mbias_ref)):
        vec_ref[i : i + 1, :] = ref[...]
    cols[...] = vec_ref[...].T
    locate(
        senders_ref[:, pl.ds(pl.multiple_of(me * share, share), share)],
        receivers_ref[...], count_ref[0, 0], near_ref, send_ref, nodes, tiles * rows, lon,
    )
    send_ref[2:3, :] = near_ref[:, pl.ds(pl.multiple_of(me * share, share), share)]
    b1, gain = cols[:, 0:1] * 0.5, cols[:, 1:2]
    gathered[...] = jnp.zeros_like(gathered)
    assigned[mine, :] = edge_ref[:, pl.ds(pl.multiple_of(me * share, share), share)]
    nodes_all[mine, :] = mesh_ref[...]
    pl.semaphore_wait(barrier, len(around))

    def remote(source, target, send_sem, recv_sem, offset):
        return pltpu.make_async_remote_copy(
            src_ref=source, dst_ref=target, send_sem=send_sem, recv_sem=recv_sem,
            device_id=partner(*offset), device_id_type=MESH,
        )

    spread = []
    for k in range(1, layers):
        peer = lax.rem(me + k, layers)
        theirs = pl.ds(pl.multiple_of(peer * share, share), share)
        spread.append(
            remote(edge_ref.at[:, theirs], assigned.at[mine, :], z_send.at[0, k], z_recv.at[0, k], (0, 0, k))
        )
        spread.append(
            remote(mesh_ref, nodes_all.at[mine, :], z_send.at[1, k], z_recv.at[1, k], (0, 0, k))
        )
    for copy in spread:
        copy.start()

    def widen(t, carry):
        pltpu.make_async_copy(
            x_hbm.at[:, pl.ds(t * rows, rows), :], x_ref.at[t], x_sem.at[t]
        ).wait()
        wide[t, pl.ds(0, channels * rows), :] = x_ref[t].astype(F32).reshape(channels * rows, lon)
        wide[t, pl.ds(channels * rows, (padded - channels) * rows), :] = jnp.zeros(
            ((padded - channels) * rows, lon), F32
        )
        lanes = lax.broadcasted_iota(jnp.int32, (padded, lon), 1) // HALO
        left = jnp.zeros((padded, lon), F32)
        right = jnp.zeros((padded, lon), F32)
        for j in range(rows):
            row = wide[t, pl.ds(j, padded, stride=rows), :]
            here = lanes == j
            left = jnp.where(here, row if j == 0 else pltpu.roll(row, j * HALO, 1), left)
            turn = (j * HALO + HALO) % lon
            right = jnp.where(here, row if turn == 0 else pltpu.roll(row, turn, 1), right)
        cols_send[0, t] = left.astype(BF16)
        cols_send[1, t] = right.astype(BF16)
        return carry

    lax.fori_loop(0, tiles, widen, 0)
    for j in range(HALO):
        at = pl.ds(j * lon, lon)
        rows_send[0, :, at] = wide[0, pl.ds(j, padded, stride=rows), :].astype(BF16)
        rows_send[1, :, at] = wide[
            tiles - 1, pl.ds(rows - HALO + j, padded, stride=rows), :
        ].astype(BF16)

    def first_layer(t, group):
        cells = jnp.concatenate(
            [wide[t, pl.ds(group * GROUP + r, padded, stride=rows), :] for r in range(GROUP)],
            axis=1,
        ).astype(BF16)
        half = jnp.dot(w1[...], cells, preferred_element_type=F32) + b1
        return cells, half_silu(half).astype(BF16)

    def embed(t):
        own_gain = cols[mine, 1:2]
        cells, hidden = first_layer(t, 0)
        for group in range(rows // GROUP):
            slot = group % 2
            pre_ref[slot] = jnp.dot(w2_ref[...], hidden, preferred_element_type=F32)
            pick = onehot_of(send_ref[0:1, :], (t * rows + group * GROUP) * lon, GROUP * lon)
            gathered[...] += jnp.dot(cells, pick, preferred_element_type=F32)
            if (group + 1) * GROUP < rows:
                cells, hidden = first_layer(t, group + 1)
            average, scale = centre(pre_ref[slot])
            own = (pre_ref[slot, mine, :] - average) * scale * own_gain
            for r in range(GROUP):
                out_wide[pl.ds(group * GROUP + r, shard, stride=rows), :] = own[
                    :, r * lon : (r + 1) * lon
                ]
        stage[t] = out_wide[...].reshape(shard, rows, lon).astype(BF16)

    def store(t):
        return pltpu.make_async_copy(
            stage.at[t], out_hbm.at[:, pl.ds(t * rows, rows), :], out_sem.at[t]
        )

    halo = [
        remote(rows_send.at[1], rows_recv.at[0], halo_send.at[0], halo_recv.at[0], (1, 0, 0)),
        remote(rows_send.at[0], rows_recv.at[1], halo_send.at[1], halo_recv.at[1], (-1, 0, 0)),
        remote(cols_send.at[1], cols_recv.at[0], halo_send.at[2], halo_recv.at[2], (0, 1, 0)),
        remote(cols_send.at[0], cols_recv.at[1], halo_send.at[3], halo_recv.at[3], (0, -1, 0)),
    ]
    for i, (dx, dy) in enumerate(diagonals):
        halo.append(
            remote(
                cols_send.at[1 if dy > 0 else 0, tiles - 1 if dx > 0 else 0],
                corner_recv.at[i], halo_send.at[4 + i], halo_recv.at[4 + i], (dx, dy, 0),
            )
        )
    for copy in halo:
        copy.start()

    def advance(t, carry):
        embed(t)
        store(t).start()
        return carry

    lax.fori_loop(0, tiles, advance, 0)

    for copy in halo:
        copy.wait()
    picked = gathered[...]
    first = 0
    pieces = [rows_recv[0], rows_recv[1]]
    pieces += [cols_recv[side, t] for side in range(2) for t in range(tiles)]
    pieces += [corner_recv[i] for i in range(4)]
    for piece in pieces:
        pick = onehot_of(send_ref[1:2, :], first, piece.shape[1])
        picked = picked + jnp.dot(piece, pick, preferred_element_type=F32)
        first += piece.shape[1]
    half = jnp.dot(w1[...], picked.astype(BF16), preferred_element_type=F32) + b1
    pre = jnp.dot(w2_ref[...], half_silu(half).astype(BF16), preferred_element_type=F32)
    average, scale = centre(pre)
    sender = ((pre - average) * scale * gain).astype(BF16)
    for copy in spread:
        copy.wait()
    onehot = onehot_of(send_ref[2:3, :], 0, nodes)
    mesh_cols = jnp.dot(nodes_all[...], onehot, preferred_element_type=F32).astype(BF16)
    for copy in weights:
        copy.wait()
    half = jnp.dot(e1_ref[:, :latent], assigned[...], preferred_element_type=F32)
    half = half + jnp.dot(e1_ref[:, latent : 2 * latent], sender, preferred_element_type=F32)
    half = half + jnp.dot(e1_ref[:, 2 * latent :], mesh_cols, preferred_element_type=F32)
    hidden = half_silu((half + cols[:, 2:3]) * 0.5).astype(BF16)
    second = jnp.dot(e2_ref[...], hidden, preferred_element_type=F32)
    average, scale = centre(second)
    message = (
        assigned[...].astype(F32) + (second - average) * scale * cols[:, 3:4] + cols[:, 4:5]
    ).astype(BF16)
    last = (((1,), (1,)), ((), ()))
    totals[...] = lax.dot_general(message, onehot, last, preferred_element_type=F32)
    parts[0] = totals[mine, :]
    exchange = []
    for k in range(1, layers):
        peer = lax.rem(me + k, layers)
        theirs = pl.ds(pl.multiple_of(peer * shard, shard), shard)
        exchange.append(
            remote(totals.at[theirs, :], parts.at[k], z_send.at[2, k], z_recv.at[2, k], (0, 0, k))
        )
    for copy in exchange:
        copy.start()
    degree = jnp.zeros((8, nodes), F32)
    for start in range(0, slots, share):
        chunk = onehot_of(near_ref[:, start : start + share], 0, nodes)
        ones = jnp.ones((8, share), BF16)
        degree = degree + lax.dot_general(ones, chunk, last, preferred_element_type=F32)
    scale = jnp.maximum(degree[:1], 1.0)
    for copy in exchange:
        copy.wait()
    total = parts[0]
    for k in range(1, layers):
        total = total + parts[k]
    mean_ref[...] = total / scale
    for t in range(tiles):
        store(t).wait()


def on_device(
    grid_inputs,
    embed_w1,
    embed_b1,
    embed_w2,
    embed_gain,
    edge_w1,
    edge_b1,
    edge_w2,
    message_gain,
    message_bias,
    mesh_latent,
    edge_latent,
    senders,
    receivers,
    edge_counts,
):
    latent = embed_w2.shape[0]
    channels, lat, lon = grid_inputs.shape
    shard = mesh_latent.shape[0]
    nodes = mesh_latent.shape[3]
    slots = edge_latent.shape[3]
    layers = lax.axis_size("gz")
    share = slots // layers
    strip = HALO * lon
    padded = -(-channels // 16) * 16
    tiles = lat // ROWS

    vmem = pl.BlockSpec(memory_space=pltpu.VMEM)
    hbm = pl.BlockSpec(memory_space=pl.ANY)
    scratch = [
        ((tiles, channels, ROWS, lon), BF16),
        ((tiles, padded * ROWS, lon), F32),
        ((latent, padded), BF16),
        ((latent, 8), F32),
        (edge_w1.shape, BF16),
        (edge_w2.shape, BF16),
        ((-(-padded // 128) * 128, latent), F32),
        ((8, latent), F32),
        ((1, slots), jnp.int32),
        ((8, share), jnp.int32),
        ((padded, share), F32),
        ((2, latent, GROUP * lon), F32),
        ((shard * ROWS, lon), F32),
        ((tiles, shard, ROWS, lon), BF16),
        ((2, padded, strip), BF16),
        ((2, tiles, padded, lon), BF16),
        ((2, padded, strip), BF16),
        ((2, tiles, padded, lon), BF16),
        ((4, padded, lon), BF16),
        ((latent, share), BF16),
        ((latent, nodes), BF16),
        ((latent, nodes), F32),
        ((layers, shard, nodes), F32),
    ]
    sems = [(tiles,), (tiles,), (2,), (8,), (8,), (3, layers), (3, layers)]
    smem = pl.BlockSpec(memory_space=pltpu.SMEM)
    line = lambda v: v.reshape(1, v.size)
    mesh_own = mesh_latent[:, 0, 0, :]
    grid_out, mean = pl.pallas_call(
        kernel,
        in_specs=[hbm, vmem, vmem, hbm, hbm] + [vmem] * 9 + [smem],
        out_specs=[hbm, vmem],
        out_shape=[
            jax.ShapeDtypeStruct((shard, lat, lon), BF16),
            jax.ShapeDtypeStruct((shard, nodes), F32),
        ],
        scratch_shapes=[pltpu.VMEM(s, d) for s, d in scratch]
        + [pltpu.SemaphoreType.DMA(s) for s in sems],
        compiler_params=pltpu.CompilerParams(
            collective_id=0, has_side_effects=True, vmem_limit_bytes=60 * 1024 * 1024
        ),
    )(
        grid_inputs, embed_w1.T, embed_w2, edge_w1, edge_w2,
        line(embed_b1), line(embed_gain), line(edge_b1), line(message_gain), line(message_bias),
        mesh_own, edge_latent[:, 0, 0, :], line(senders), line(receivers), edge_counts,
    )
    mesh_out = (mesh_own.astype(F32) + mean).astype(BF16)
    return (mesh_out.reshape(shard, 1, 1, nodes), grid_out)


def solution(mesh):
    return jax.shard_map(
        on_device,
        mesh=mesh,
        in_specs=(
            P(None, "gx", "gy"),
            P(),
            P(),
            P(),
            P(),
            P(),
            P(),
            P(),
            P(),
            P(),
            P("gz", "gx", "gy", None),
            P("gz", "gx", "gy", None),
            P("gx", "gy", None),
            P("gx", "gy", None),
            P("gx", "gy"),
        ),
        out_specs=(P("gz", "gx", "gy", None), P("gz", "gx", "gy")),
        check_vma=False,
    )
```

profile of v0, /device:TPU:0, one launch (start us, length us, event | category | flops | bytes accessed | tf_op | source)
XLA Modules:
  0.0 49.7 jit_solution(9573093072107779466)
XLA Ops:
  1.3 0.0 copy-start
  1.3 43.8 %shard_map.158 = (bf16[128,64,128]{2,1,0:T(8,128)(2,1)}, f32[128,256]{1,0:T(8,128)}) custom-call(bf16[186,64,128]{2,1,0:T(8,128)(2,1)} %x_hbm.1, bf16[186,512]{1,0:T(8,128)(2,1)} %bitcast.15, bf16[512,512]{1,0:T(8,128)(2,1)} %w2_ref.1, bf16[512,1536]{1,0:T(8,128)(2,1)} %e1_hbm.1, bf16[512,512]{1,0:T(8,128)(2,1)} %e2_hbm.1, f32[1,512]{1,0:T(1,128)} %bitcast.18, ...), custom_call_target="tpu_custom_call" | custom-call | tf_op jit(solution)/shard_map/pallas_call | solution.py:353
  45.1 0.0 copy-done
  45.1 1.5 %fusion = bf16[128,1,1,256]{3,0,2,1:T(8,128)(2,1)} fusion(f32[128,256]{1,0:T(8,128)} %get-tuple-element.4, bf16[128,1,1,256]{3,0,2,1:T(8,128)(2,1)S(1)} %copy-done), kind=kLoop, calls=%fused_computation.1 | loop fusion | flops 98304 | bytes 262144 | tf_op jit(solution)/shard_map/reshape | solution.py:372
  46.7 3.1 %copy.19 = bf16[128,64,128]{2,1,0:T(8,128)(2,1)} copy(bf16[128,64,128]{2,1,0:T(8,128)(2,1)} %get-tuple-element.9) | data formatting | bytes 4194304
Async XLA Ops:
  1.3 43.8 %copy-start = (bf16[128,1,1,256]{3,0,2,1:T(8,128)(2,1)S(1)}, bf16[128,1,1,256]{3,0,2,1:T(8,128)(2,1)}, u32[]{:S(2)}) copy-start(bf16[128,1,1,256]{3,0,2,1:T(8,128)(2,1)} %param.25) | copy-start | bytes 196612
where the time goes:
time: 50.4 us; the launch traced here: 49.7 us
  Pallas kernels  43.8 us (87%)
  local copies, waits for them, and re-layouts  3.08 us (6%)
  other arithmetic  1.55 us (3%)
  between operations  1.31 us (3%)
    pallas_call x1, Pallas kernels, on_device(): pl.pallas_call(kernel, in_specs=[hbm, vmem, vmem, hbm, hbm] + [vmem] * 9...  43.8 us
    unnamed x3, local copies, waits for them, and re-layouts  3.08 us
    reshape x1, other arithmetic, on_device(): return (mesh_out.reshape(shard, 1, 1, nodes), grid_out)  1.55 us

commit v1 on v0

--- a/solution.py
+++ b/solution.py
@@ -80,11 +80,11 @@
 def kernel(
     x_hbm, w1_ref, w2_ref, e1_hbm, e2_hbm, b1_ref, gain_ref, eb1_ref, mgain_ref, mbias_ref,
     mesh_ref, edge_ref, senders_ref, receivers_ref, count_ref,
-    out_hbm, mean_ref,
-    x_ref, wide, w1, cols, e1_ref, e2_ref, w1_wide, vec_ref, near_ref, send_ref, gathered, pre_ref, out_wide, stage,
+    stage, mean_ref,
+    x_ref, wide, w1, cols, e1_ref, e2_ref, w1_wide, vec_ref, near_ref, send_ref, gathered, pre_ref, out_wide,
     rows_send, cols_send, rows_recv, cols_recv, corner_recv,
-    assigned, nodes_all, totals, parts,
-    x_sem, out_sem, w_sem, halo_send, halo_recv, z_send, z_recv,
+    assigned, nodes_all, totals, sent, parts,
+    x_sem, w_sem, halo_send, halo_recv, z_send, z_recv,
 ):
     tiles, channels, rows, lon = x_ref.shape
     padded = w1.shape[1]
@@ -205,11 +205,6 @@
                 ]
         stage[t] = out_wide[...].reshape(shard, rows, lon).astype(BF16)
 
-    def store(t):
-        return pltpu.make_async_copy(
-            stage.at[t], out_hbm.at[:, pl.ds(t * rows, rows), :], out_sem.at[t]
-        )
-
     halo = [
         remote(rows_send.at[1], rows_recv.at[0], halo_send.at[0], halo_recv.at[0], (1, 0, 0)),
         remote(rows_send.at[0], rows_recv.at[1], halo_send.at[1], halo_recv.at[1], (-1, 0, 0)),
@@ -228,7 +223,6 @@
 
     def advance(t, carry):
         embed(t)
-        store(t).start()
         return carry
 
     lax.fori_loop(0, tiles, advance, 0)
@@ -265,13 +259,13 @@
     ).astype(BF16)
     last = (((1,), (1,)), ((), ()))
     totals[...] = lax.dot_general(message, onehot, last, preferred_element_type=F32)
-    parts[0] = totals[mine, :]
+    sent[...] = totals[...].astype(BF16)
     exchange = []
     for k in range(1, layers):
         peer = lax.rem(me + k, layers)
         theirs = pl.ds(pl.multiple_of(peer * shard, shard), shard)
         exchange.append(
-            remote(totals.at[theirs, :], parts.at[k], z_send.at[2, k], z_recv.at[2, k], (0, 0, k))
+            remote(sent.at[theirs, :], parts.at[k], z_send.at[2, k], z_recv.at[2, k], (0, 0, k))
         )
     for copy in exchange:
         copy.start()
@@ -283,12 +277,23 @@
     scale = jnp.maximum(degree[:1], 1.0)
     for copy in exchange:
         copy.wait()
-    total = parts[0]
+    total = totals[mine, :]
     for k in range(1, layers):
-        total = total + parts[k]
-    mean_ref[...] = total / scale
-    for t in range(tiles):
-        store(t).wait()
+        total = total + parts[k].astype(F32)
+    mean_ref[...] = (mesh_ref[...].astype(F32) + total / scale).astype(BF16)
+
+
+def finish(stage, mesh_ref, grid_out, mesh_out, sem):
+    tiles, _, rows, _ = stage.shape
+    copies = [
+        pltpu.make_async_copy(stage.at[t], grid_out.at[:, pl.ds(t * rows, rows), :], sem.at[t])
+        for t in range(tiles)
+    ]
+    copies.append(pltpu.make_async_copy(mesh_ref, mesh_out, sem.at[tiles]))
+    for copy in copies:
+        copy.start()
+    for copy in copies:
+        copy.wait()
 
 
 def on_device(
@@ -335,7 +340,6 @@
         ((padded, share), F32),
         ((2, latent, GROUP * lon), F32),
         ((shard * ROWS, lon), F32),
-        ((tiles, shard, ROWS, lon), BF16),
         ((2, padded, strip), BF16),
         ((2, tiles, padded, lon), BF16),
         ((2, padded, strip), BF16),
@@ -344,19 +348,20 @@
         ((latent, share), BF16),
         ((latent, nodes), BF16),
         ((latent, nodes), F32),
-        ((layers, shard, nodes), F32),
+        ((latent, nodes), BF16),
+        ((layers, shard, nodes), BF16),
     ]
-    sems = [(tiles,), (tiles,), (2,), (8,), (8,), (3, layers), (3, layers)]
+    sems = [(tiles,), (2,), (8,), (8,), (3, layers), (3, layers)]
     smem = pl.BlockSpec(memory_space=pltpu.SMEM)
     line = lambda v: v.reshape(1, v.size)
     mesh_own = mesh_latent[:, 0, 0, :]
-    grid_out, mean = pl.pallas_call(
+    stage, mean = pl.pallas_call(
         kernel,
         in_specs=[hbm, vmem, vmem, hbm, hbm] + [vmem] * 9 + [smem],
-        out_specs=[hbm, vmem],
+        out_specs=[vmem, vmem],
         out_shape=[
-            jax.ShapeDtypeStruct((shard, lat, lon), BF16),
-            jax.ShapeDtypeStruct((shard, nodes), F32),
+            pltpu.VMEM((tiles, shard, ROWS, lon), BF16),
+            pltpu.VMEM((shard, nodes), BF16),
         ],
         scratch_shapes=[pltpu.VMEM(s, d) for s, d in scratch]
         + [pltpu.SemaphoreType.DMA(s) for s in sems],
@@ -368,7 +373,17 @@
         line(embed_b1), line(embed_gain), line(edge_b1), line(message_gain), line(message_bias),
         mesh_own, edge_latent[:, 0, 0, :], line(senders), line(receivers), edge_counts,
     )
-    mesh_out = (mesh_own.astype(F32) + mean).astype(BF16)
+    grid_out, mesh_out = pl.pallas_call(
+        finish,
+        in_specs=[vmem, vmem],
+        out_specs=[hbm, hbm],
+        out_shape=[
+            jax.ShapeDtypeStruct((shard, lat, lon), BF16),
+            jax.ShapeDtypeStruct((shard, nodes), BF16),
+        ],
+        scratch_shapes=[pltpu.SemaphoreType.DMA((tiles + 1,))],
+        compiler_params=pltpu.CompilerParams(vmem_limit_bytes=1024 * 1024),
+    )(pltpu.with_memory_space_constraint(stage, pltpu.VMEM), pltpu.with_memory_space_constraint(mean, pltpu.VMEM))
     return (mesh_out.reshape(shard, 1, 1, nodes), grid_out)
 
 

time: 50.4 us -> 42.5 us (0.84); the launches traced: 49.7 us -> 42.4 us
  local copies, waits for them, and re-layouts: 3.08 us -> 0 us
  Pallas kernels: 43.8 us -> 41.1 us
  other arithmetic: 1.55 us -> 0 us
    pallas_call x1, Pallas kernels: 43.8 us -> 39.7 us  [on_device(): pl.pallas_call(kernel, in_specs=[hbm, vmem, vmem, hbm, hbm] + [vmem] * 9...]
    unnamed x3 -> x0, local copies, waits for them, and re-layouts: 3.08 us -> none
    reshape x1 -> x0, other arithmetic: 1.55 us -> none  [on_device(): return (mesh_out.reshape(shard, 1, 1, nodes), grid_out)]
    pallas_call x0 -> x1, Pallas kernels: none -> 1.37 us  [on_device(): pl.pallas_call(finish, in_specs=[vmem, vmem], out_specs=[hbm, hbm], out_s...]
where the time goes in v1:
time: 42.5 us; the launch traced here: 42.4 us
  Pallas kernels  41.1 us (97%)
  between operations  1.29 us (3%)
    pallas_call x1, Pallas kernels, on_device(): pl.pallas_call(kernel, in_specs=[hbm, vmem, vmem, hbm, hbm] + [vmem] * 9...  39.7 us
    pallas_call x1, Pallas kernels, on_device(): pl.pallas_call(finish, in_specs=[vmem, vmem], out_specs=[hbm, hbm], out_s...  1.37 us

profile of v1, /device:TPU:0, one launch (start us, length us, event | category | flops | bytes accessed | tf_op | source)
XLA Modules:
  0.0 42.4 jit_solution(1644681221975988798)
XLA Ops:
  1.3 39.7 %shard_map.158 = (bf16[4,128,16,128]{3,2,1,0:T(8,128)(2,1)S(1)}, bf16[128,256]{1,0:T(8,128)(2,1)S(1)}) custom-call(bf16[186,64,128]{2,1,0:T(8,128)(2,1)} %x_hbm.1, bf16[186,512]{1,0:T(8,128)(2,1)} %bitcast.12, bf16[512,512]{1,0:T(8,128)(2,1)} %w2_ref.1, bf16[512,1536]{1,0:T(8,128)(2,1)} %e1_hbm.1, bf16[512,512]{1,0:T(8,128)(2,1)} %e2_hbm.1, ...), custom_call_target="tpu_custom_call" | custom-call | tf_op jit(solution)/shard_map/pallas_call | solution.py:358
  41.0 1.4 %shard_map.159 = (bf16[128,64,128]{2,1,0:T(8,128)(2,1)}, bf16[128,256]{1,0:T(8,128)(2,1)}) custom-call(bf16[4,128,16,128]{3,2,1,0:T(8,128)(2,1)S(1)} %get-tuple-element.6.stage, bf16[128,256]{1,0:T(8,128)(2,1)S(1)} %get-tuple-element.7.mesh_ref), custom_call_target="tpu_custom_call" | custom-call | tf_op jit(solution)/shard_map/pallas_call | solution.py:376

commit v2 on v1

v2 whole, which is shorter than its diff:
```python
import jax
import jax.numpy as jnp
from jax import lax
from jax.experimental import pallas as pl
from jax.experimental.pallas import tpu as pltpu
from jax.sharding import PartitionSpec as P

HALO = 8
ROWS = 16
GROUP = 4
EARLY = 2

epsilon = 1e-05
F32 = jnp.float32
BF16 = jnp.bfloat16
MESH = pl.DeviceIdType.MESH


def half_silu(half):
    return half + half * jnp.tanh(half)


def inverse_spread(values):
    return lax.rsqrt(jnp.mean(values * values, axis=0, keepdims=True) + epsilon)


def onehot_of(index_row, first, count):
    ids = lax.broadcasted_iota(jnp.int32, (count, index_row.shape[1]), 0)
    return jnp.where(ids == index_row - first, 1.0, 0.0).astype(BF16)


def partner(dx, dy, dz):
    ids = {}
    for axis, step in (("gx", dx), ("gy", dy), ("gz", dz)):
        size = lax.axis_size(axis)
        ids[axis] = lax.rem(lax.axis_index(axis) + (step + size), size)
    return ids


def remote(source, target, send_sem, recv_sem, offset):
    return pltpu.make_async_remote_copy(
        src_ref=source, dst_ref=target, send_sem=send_sem, recv_sem=recv_sem,
        device_id=partner(*offset), device_id_type=MESH,
    )


def split(values, size):
    if size & (size - 1) == 0:
        return lax.shift_right_logical(values, size.bit_length() - 1), values & (size - 1)
    return values // size, values % size


def locate(send, lat, lon, sides):
    band = lax.axis_index("gx")
    sector = lax.axis_index("gy")
    lon_total = lon * lax.axis_size("gy")
    row, column = split(send, lon_total)
    row = row - band * lat
    column = split(column - sector * lon + (HALO + lon_total), lon_total)[1] - HALO
    above, below = row < 0, row >= lat
    west, east = column < 0, column >= lon
    outside_row = jnp.where(above, 1, jnp.where(below, 1, 0))
    outside_column = jnp.where(west, 1, jnp.where(east, 1, 0))
    inside = outside_row + outside_column == 0
    strip = HALO * lon
    row_index = jnp.where(above, row + HALO, row - lat + HALO) * lon + column
    pair = 2 * HALO
    beside = jnp.where(west, column + HALO, column - lon + HALO)
    tall = lat * pair
    side = jnp.where(west, 0, sides - 1)
    column_index = 2 * strip + side * tall + row * pair + beside
    corner_row = jnp.where(above, row + HALO, row - lat)
    corner = jnp.where(above, 0, 1) * sides + side
    corner_index = 2 * strip + sides * tall + corner * lon + corner_row * pair + beside
    halo = jnp.where(
        outside_column == 0,
        jnp.where(outside_row == 0, -1, row_index),
        jnp.where(outside_row == 0, column_index, corner_index),
    )
    return jnp.where(inside, row, -1), jnp.where(inside, column, -1), halo


def kernel(
    x_hbm, w1_hbm, w2_hbm, e1_hbm, e2_hbm, b1_hbm, gain_hbm, eb1_hbm, mgain_hbm, mbias_hbm,
    mesh_hbm, edge_hbm, senders_hbm, receivers_hbm, count_hbm,
    stage, mean_ref,
    x_ref, wide, xw, w1_in, w1_wide, w1, w2_in, w2, e1_ref, e2_in, e2_ref, vec_ref, cols,
    senders_ref, receivers_ref, count_ref, near_ref, place_ref, cmask, gathered, out_wide, sender_ref, half_ref,
    cols_send, rows_recv, rows_all, cols_recv, corner_recv,
    assigned, nodes_all, totals, sent, parts, degree_ref,
    x_sem, in_sem, halo_send, halo_recv, z_send, z_recv,
):
    tiles, channels, rows, lon = x_ref.shape
    lat = tiles * rows
    padded = w1.shape[1]
    latent, share = assigned.shape
    shard, nodes = parts.shape[1:]
    slots = receivers_ref.shape[1]
    layers = slots // share
    sides = cols_recv.shape[0]
    groups = rows // GROUP
    me = lax.axis_index("gz")
    mine = pl.ds(pl.multiple_of(me * shard, shard), shard)
    own_edges = pl.ds(pl.multiple_of(me * share, share), share)

    steps = (1,) if sides == 1 else (-1, 1)
    around = [(1, 0, 0), (-1, 0, 0)] + [(0, dy, 0) for dy in steps]
    around += [(dx, dy, 0) for dx in (1, -1) for dy in steps]
    around += [(0, 0, k) for k in range(1, layers)]
    barrier = pltpu.get_barrier_semaphore()
    for offset in around:
        pl.semaphore_signal(barrier, inc=1, device_id=partner(*offset), device_id_type=MESH)
    local = [
        (w1_hbm, w1_in), (w2_hbm, w2_in), (senders_hbm, senders_ref), (receivers_hbm, receivers_ref),
        (count_hbm, count_ref), (e1_hbm, e1_ref), (e2_hbm, e2_in),
        (mesh_hbm, nodes_all.at[mine, :]), (edge_hbm.at[:, own_edges], assigned.at[mine, :]),
    ]
    local += [
        (ref, vec_ref.at[pl.ds(i, 1), :])
        for i, ref in enumerate((b1_hbm, gain_hbm, eb1_hbm, mgain_hbm, mbias_hbm))
    ]
    local = [pltpu.make_async_copy(a, b, in_sem.at[i]) for i, (a, b) in enumerate(local)]
    loads = [
        pltpu.make_async_copy(x_hbm.at[:, pl.ds(t * rows, rows), :], x_ref.at[t], x_sem.at[t])
        for t in range(tiles)
    ]
    for load in loads + local:
        load.start()
    pl.semaphore_wait(barrier, len(around))

    spread = []
    for k in range(1, layers):
        peer = lax.rem(me + k, layers)
        theirs = pl.ds(pl.multiple_of(peer * share, share), share)
        spread.append(
            remote(mesh_hbm, nodes_all.at[mine, :], z_send.at[1, k], z_recv.at[1, k], (0, 0, k))
        )
        spread.append(
            remote(edge_hbm.at[:, theirs], assigned.at[mine, :], z_send.at[0, k], z_recv.at[0, k], (0, 0, k))
        )
    halo = [
        remote(x_hbm.at[:, pl.ds(lat - HALO, HALO), :], rows_recv.at[0], halo_send.at[0], halo_recv.at[0], (1, 0, 0)),
        remote(x_hbm.at[:, pl.ds(0, HALO), :], rows_recv.at[1], halo_send.at[1], halo_recv.at[1], (-1, 0, 0)),
    ]
    for copy in spread + halo:
        copy.start()

    wide[...] = jnp.zeros_like(wide)

    def relay(source, slot, height):
        wide[slot, pl.ds(0, channels * height), :] = source.astype(F32).reshape(channels * height, lon)

        def row(j):
            return wide[slot, pl.ds(j, padded, stride=height), :].astype(BF16)

        return row

    lanes = lax.broadcasted_iota(jnp.int32, (padded, lon), 1) // (2 * HALO)

    def widen(t, carry):
        pltpu.make_async_copy(
            x_hbm.at[:, pl.ds(t * rows, rows), :], x_ref.at[t], x_sem.at[t]
        ).wait()
        row_of = relay(x_ref[t], 0, rows)
        for half in range(rows // HALO):
            beside = jnp.zeros((padded, lon), F32)
            for j in range(HALO):
                r = half * HALO + j
                value = wide[0, pl.ds(r, padded, stride=rows), :]
                xw[t * groups + r // GROUP, :, (r % GROUP) * lon : (r % GROUP + 1) * lon] = value.astype(BF16)
                turn = (2 * j * HALO + HALO) % lon
                beside = jnp.where(lanes == j, pltpu.roll(value, turn, 1), beside)
            cols_send[t * (rows // HALO) + half] = beside.astype(BF16)
        return carry

    lax.fori_loop(0, tiles, widen, 0)
    for i, dy in enumerate(steps):
        slot = sides - 1 - i
        halo.append(
            remote(cols_send, cols_recv.at[slot], halo_send.at[2 + i], halo_recv.at[2 + i], (0, dy, 0))
        )
        for n, dx in enumerate((1, -1)):
            block = cols_send.at[lat // HALO - 1 if dx > 0 else 0]
            at = 4 + 2 * n + i
            halo.append(
                remote(block, corner_recv.at[n, slot], halo_send.at[at], halo_recv.at[at], (dx, dy, 0))
            )
    for copy in halo[2:]:
        copy.start()

    for copy in local:
        copy.wait()
    w1_wide[...] = jnp.zeros_like(w1_wide)
    w1_wide[:channels, :] = w1_in[...].astype(F32) * 0.5
    w1[...] = w1_wide[...].T[:, :padded].astype(BF16)
    cols[...] = vec_ref[...].T
    average = jnp.mean(w2_in[...].astype(F32), axis=0, keepdims=True)
    for k in range(layers):
        block = pl.ds(pl.multiple_of(lax.rem(me + k, layers) * shard, shard), shard)
        w2[pl.ds(k * shard, shard), :] = (w2_in[block, :].astype(F32) - average).astype(BF16)
    e2_wide = e2_in[...].astype(F32)
    e2_ref[...] = (e2_wide - jnp.mean(e2_wide, axis=0, keepdims=True)).astype(BF16)
    tile = lax.axis_index("gx") * lax.axis_size("gy") + lax.axis_index("gy")
    slot_ids = lax.broadcasted_iota(jnp.int32, (1, slots), 1)
    near_ref[...] = jnp.where(slot_ids < count_ref[...], receivers_ref[...] - tile * nodes, -1)
    own_row, own_column, own_halo = locate(senders_ref[:, own_edges], lat, lon, sides)
    place_ref[0:1, :] = own_row
    place_ref[1:2, :] = own_halo
    place_ref[2:3, :] = near_ref[:, own_edges]
    cmask[...] = onehot_of(own_column, 0, lon)
    gathered[...] = jnp.zeros_like(gathered)
    b1 = cols[:, 0:1] * 0.5

    def pick_rows(first, count):
        picks = []
        for r in range(count):
            here = jnp.where(place_ref[0:1, :] == first + r, 1.0, 0.0)
            here = jnp.broadcast_to(here, (16, share)).astype(BF16)
            picks.append((cmask[...].reshape(lon // 16, 16, share) * here[None]).reshape(lon, share))
        return jnp.concatenate(picks, axis=0)

    def gather(g, carry):
        gathered[...] += jnp.dot(xw[g], pick_rows(g * GROUP, GROUP), preferred_element_type=F32)
        return carry

    lax.fori_loop(0, tiles * groups, gather, 0)

    def first_layer(g):
        half = jnp.dot(w1[...], xw[g], preferred_element_type=F32) + b1
        return half_silu(half).astype(BF16)

    def embed(t, carry):
        own_gain = cols[mine, 1:2]
        hidden = first_layer(t * groups)
        for group in range(groups):
            pre = jnp.dot(w2[...], hidden, preferred_element_type=F32)
            if group + 1 < groups:
                hidden = first_layer(t * groups + group + 1)
            own = pre[:shard, :] * inverse_spread(pre) * own_gain
            for r in range(GROUP):
                out_wide[pl.ds(group * GROUP + r, shard, stride=rows), :] = own[
                    :, r * lon : (r + 1) * lon
                ]
        stage[t] = out_wide[...].reshape(shard, rows, lon).astype(BF16)
        return carry

    lax.fori_loop(0, EARLY, embed, 0)

    last = (((1,), (1,)), ((), ()))
    degree = jnp.zeros((8, nodes), F32)
    for start in range(0, slots, share):
        chunk = onehot_of(near_ref[:, start : start + share], 0, nodes)
        ones = jnp.ones((8, share), BF16)
        degree = degree + lax.dot_general(ones, chunk, last, preferred_element_type=F32)
    degree_ref[...] = jnp.maximum(degree, 1.0)

    for copy in halo:
        copy.wait()
    for i in range(2):
        row_of = relay(rows_recv[i], 0, HALO)
        for j in range(HALO):
            rows_all[i, :, j * lon : (j + 1) * lon] = row_of(j)
    picked = gathered[...]
    pieces = [rows_all[0], rows_all[1]]
    for side in range(sides):
        pieces.append(jnp.concatenate([cols_recv[side, b] for b in range(lat // HALO)], axis=1))
    pieces.append(jnp.concatenate([corner_recv[n, side] for n in range(2) for side in range(sides)], axis=1))
    first = 0
    for piece in pieces:
        pick = onehot_of(place_ref[1:2, :], first, piece.shape[1])
        picked = picked + jnp.dot(piece, pick, preferred_element_type=F32)
        first += piece.shape[1]
    half = jnp.dot(w1[...], picked.astype(BF16), preferred_element_type=F32) + b1
    hidden = half_silu(half).astype(BF16)
    pre = jnp.dot(w2[...], hidden, preferred_element_type=F32)
    scale = inverse_spread(pre)
    for k in range(layers):
        block = pl.ds(pl.multiple_of(lax.rem(me + k, layers) * shard, shard), shard)
        part = pre[k * shard : (k + 1) * shard, :] * scale * cols[block, 1:2]
        sender_ref[block, :] = part.astype(BF16)
    half_ref[...] = jnp.dot(e1_ref[:, latent : 2 * latent], sender_ref[...], preferred_element_type=F32)

    for copy in spread:
        copy.wait()
    onehot = onehot_of(place_ref[2:3, :], 0, nodes)
    mesh_cols = jnp.dot(nodes_all[...], onehot, preferred_element_type=F32).astype(BF16)
    half = half_ref[...] + jnp.dot(e1_ref[:, :latent], assigned[...], preferred_element_type=F32)
    half = half + jnp.dot(e1_ref[:, 2 * latent :], mesh_cols, preferred_element_type=F32)
    hidden = half_silu((half + cols[:, 2:3]) * 0.5).astype(BF16)
    second = jnp.dot(e2_ref[...], hidden, preferred_element_type=F32)
    message = (
        assigned[...].astype(F32) + second * inverse_spread(second) * cols[:, 3:4] + cols[:, 4:5]
    ).astype(BF16)
    totals[...] = lax.dot_general(message, onehot, last, preferred_element_type=F32)
    sent[...] = totals[...].astype(BF16)
    exchange = []
    for k in range(1, layers):
        peer = lax.rem(me + k, layers)
        theirs = pl.ds(pl.multiple_of(peer * shard, shard), shard)
        exchange.append(
            remote(sent.at[theirs, :], parts.at[k], z_send.at[2, k], z_recv.at[2, k], (0, 0, k))
        )
    for copy in exchange:
        copy.start()

    lax.fori_loop(EARLY, tiles, embed, 0)

    for copy in exchange:
        copy.wait()
    total = totals[mine, :]
    for k in range(1, layers):
        total = total + parts[k].astype(F32)
    mean_ref[...] = (nodes_all[mine, :].astype(F32) + total / degree_ref[0:1, :]).astype(BF16)


def finish(stage, mesh_ref, grid_out, mesh_out, sem):
    tiles, _, rows, _ = stage.shape
    copies = [
        pltpu.make_async_copy(stage.at[t], grid_out.at[:, pl.ds(t * rows, rows), :], sem.at[t])
        for t in range(tiles)
    ]
    copies.append(pltpu.make_async_copy(mesh_ref, mesh_out, sem.at[tiles]))
    for copy in copies:
        copy.start()
    for copy in copies:
        copy.wait()


def on_device(
    grid_inputs,
    embed_w1,
    embed_b1,
    embed_w2,
    embed_gain,
    edge_w1,
    edge_b1,
    edge_w2,
    message_gain,
    message_bias,
    mesh_latent,
    edge_latent,
    senders,
    receivers,
    edge_counts,
):
    latent = embed_w2.shape[0]
    channels, lat, lon = grid_inputs.shape
    shard = mesh_latent.shape[0]
    nodes = mesh_latent.shape[3]
    slots = edge_latent.shape[3]
    layers = lax.axis_size("gz")
    sides = 1 if lax.axis_size("gy") == 2 else 2
    share = slots // layers
    padded = -(-channels // 16) * 16
    tiles = lat // ROWS
    I32 = jnp.int32

    vmem = pl.BlockSpec(memory_space=pltpu.VMEM)
    hbm = pl.BlockSpec(memory_space=pltpu.HBM)
    scratch = [
        ((tiles, channels, ROWS, lon), BF16),
        ((1, padded * ROWS, lon), F32),
        ((lat // GROUP, padded, GROUP * lon), BF16),
        ((channels, latent), BF16),
        ((-(-padded // 128) * 128, latent), F32),
        ((latent, padded), BF16),
        (embed_w2.shape, BF16),
        (embed_w2.shape, BF16),
        (edge_w1.shape, BF16),
        (edge_w2.shape, BF16),
        (edge_w2.shape, BF16),
        ((8, latent), F32),
        ((latent, 8), F32),
        ((1, slots), I32),
        ((1, slots), I32),
        ((1, 1), I32),
        ((1, slots), I32),
        ((8, share), I32),
        ((lon, share), BF16),
        ((padded, share), F32),
        ((shard * ROWS, lon), F32),
        ((latent, share), BF16),
        ((latent, share), F32),
        ((lat // HALO, padded, lon), BF16),
        ((2, channels, HALO, lon), BF16),
        ((2, padded, HALO * lon), BF16),
        ((sides, lat // HALO, padded, lon), BF16),
        ((2, sides, padded, lon), BF16),
        ((latent, share), BF16),
        ((latent, nodes), BF16),
        ((latent, nodes), F32),
        ((latent, nodes), BF16),
        ((layers, shard, nodes), BF16),
        ((8, nodes), F32),
    ]
    sems = [(tiles,), (14,), (8,), (8,), (3, layers), (3, layers)]
    line = lambda v: v.reshape(1, v.size)
    stage, mean = pl.pallas_call(
        kernel,
        in_specs=[hbm] * 15,
        out_specs=[vmem, vmem],
        out_shape=[
            pltpu.VMEM((tiles, shard, ROWS, lon), BF16),
            pltpu.VMEM((shard, nodes), BF16),
        ],
        scratch_shapes=[pltpu.VMEM(s, d) for s, d in scratch]
        + [pltpu.SemaphoreType.DMA(s) for s in sems],
        compiler_params=pltpu.CompilerParams(
            collective_id=0, has_side_effects=True, vmem_limit_bytes=64_860_000
        ),
    )(
        grid_inputs, embed_w1.T, embed_w2, edge_w1, edge_w2,
        line(embed_b1), line(embed_gain), line(edge_b1), line(message_gain), line(message_bias),
        mesh_latent[:, 0, 0, :], edge_latent[:, 0, 0, :], line(senders), line(receivers), edge_counts,
    )
    grid_out, mesh_out = pl.pallas_call(
        finish,
        in_specs=[vmem, vmem],
        out_specs=[hbm, hbm],
        out_shape=[
            jax.ShapeDtypeStruct((shard, lat, lon), BF16),
            jax.ShapeDtypeStruct((shard, nodes), BF16),
        ],
        scratch_shapes=[pltpu.SemaphoreType.DMA((tiles + 1,))],
        compiler_params=pltpu.CompilerParams(vmem_limit_bytes=1024 * 1024),
    )(
        pltpu.with_memory_space_constraint(stage, pltpu.VMEM),
        pltpu.with_memory_space_constraint(mean, pltpu.VMEM),
    )
    return (mesh_out.reshape(shard, 1, 1, nodes), grid_out)


def solution(mesh):
    return jax.shard_map(
        on_device,
        mesh=mesh,
        in_specs=(
            P(None, "gx", "gy"),
            P(),
            P(),
            P(),
            P(),
            P(),
            P(),
            P(),
            P(),
            P(),
            P("gz", "gx", "gy", None),
            P("gz", "gx", "gy", None),
            P("gx", "gy", None),
            P("gx", "gy", None),
            P("gx", "gy"),
        ),
        out_specs=(P("gz", "gx", "gy", None), P("gz", "gx", "gy")),
        check_vma=False,
    )
```

time: 42.5 us -> 35.7 us (0.84)
  Pallas kernels: 41.1 us -> 34.2 us
    pallas_call x1, Pallas kernels: 39.7 us -> 32.9 us  [on_device(): pl.pallas_call(kernel, in_specs=[hbm] * 15, out_specs=[vmem, vmem], out_s...]
where the time goes in v2:
time: 35.7 us; the launch traced here: 35.5 us
  Pallas kernels  34.2 us (96%)
  between operations  1.29 us (4%)
    pallas_call x1, Pallas kernels, on_device(): pl.pallas_call(kernel, in_specs=[hbm] * 15, out_specs=[vmem, vmem], out_s...  32.9 us
    pallas_call x1, Pallas kernels, on_device(): pl.pallas_call(finish, in_specs=[vmem, vmem], out_specs=[hbm, hbm], out_s...  1.37 us

profile of v2, /device:TPU:0, one launch (start us, length us, event | category | flops | bytes accessed | tf_op | source)
XLA Modules:
  0.0 35.5 jit_solution(14733839886510563251)
XLA Ops:
  1.3 32.9 %shard_map.158 = (bf16[4,128,16,128]{3,2,1,0:T(8,128)(2,1)S(1)}, bf16[128,256]{1,0:T(8,128)(2,1)S(1)}) custom-call(bf16[186,64,128]{2,1,0:T(8,128)(2,1)} %x_hbm.1, bf16[186,512]{1,0:T(8,128)(2,1)} %bitcast.12, bf16[512,512]{1,0:T(8,128)(2,1)} %w2_hbm.1, bf16[512,1536]{1,0:T(8,128)(2,1)} %e1_hbm.1, bf16[512,512]{1,0:T(8,128)(2,1)} %e2_hbm.1, ...), custom_call_target="tpu_custom_call" | custom-call | tf_op jit(solution)/shard_map/pallas_call | solution.py:398
  34.1 1.4 %shard_map.159 = (bf16[128,64,128]{2,1,0:T(8,128)(2,1)}, bf16[128,256]{1,0:T(8,128)(2,1)}) custom-call(bf16[4,128,16,128]{3,2,1,0:T(8,128)(2,1)S(1)} %get-tuple-element.6.stage, bf16[128,256]{1,0:T(8,128)(2,1)S(1)} %get-tuple-element.7.mesh_ref), custom_call_target="tpu_custom_call" | custom-call | tf_op jit(solution)/shard_map/pallas_call | solution.py:416

commit v3 on v2

--- a/solution.py
+++ b/solution.py
@@ -9,6 +9,8 @@
 ROWS = 16
 GROUP = 4
 EARLY = 2
+PARTS = 2
+REACH = 2
 
 epsilon = 1e-05
 F32 = jnp.float32
@@ -61,23 +63,19 @@
     west, east = column < 0, column >= lon
     outside_row = jnp.where(above, 1, jnp.where(below, 1, 0))
     outside_column = jnp.where(west, 1, jnp.where(east, 1, 0))
-    inside = outside_row + outside_column == 0
-    strip = HALO * lon
-    row_index = jnp.where(above, row + HALO, row - lat + HALO) * lon + column
-    pair = 2 * HALO
+    tall = lat // HALO
+    side = jnp.where(west, 0, sides - 1)
     beside = jnp.where(west, column + HALO, column - lon + HALO)
-    tall = lat * pair
-    side = jnp.where(west, 0, sides - 1)
-    column_index = 2 * strip + side * tall + row * pair + beside
-    corner_row = jnp.where(above, row + HALO, row - lat)
-    corner = jnp.where(above, 0, 1) * sides + side
-    corner_index = 2 * strip + sides * tall + corner * lon + corner_row * pair + beside
-    halo = jnp.where(
+    row_block = lat + jnp.where(above, row + HALO, row - lat + HALO)
+    column_block = lat + 2 * HALO + side * tall + lax.shift_right_arithmetic(row, HALO.bit_length() - 1)
+    corner_block = lat + 2 * HALO + sides * tall + jnp.where(above, 0, 1) * sides + side
+    block = jnp.where(
         outside_column == 0,
-        jnp.where(outside_row == 0, -1, row_index),
-        jnp.where(outside_row == 0, column_index, corner_index),
+        jnp.where(outside_row == 0, row, row_block),
+        jnp.where(outside_row == 0, column_block, corner_block),
     )
-    return jnp.where(inside, row, -1), jnp.where(inside, column, -1), halo
+    lane = jnp.where(outside_column == 0, column, (row & (HALO - 1)) * (2 * HALO) + beside)
+    return block, lane
 
 
 def kernel(
@@ -85,10 +83,10 @@
     mesh_hbm, edge_hbm, senders_hbm, receivers_hbm, count_hbm,
     stage, mean_ref,
     x_ref, wide, xw, w1_in, w1_wide, w1, w2_in, w2, e1_ref, e2_in, e2_ref, vec_ref, cols,
-    senders_ref, receivers_ref, count_ref, near_ref, place_ref, cmask, gathered, out_wide, sender_ref, half_ref,
+    senders_ref, receivers_ref, count_ref, near_ref, place_ref, cmask, out_wide, sender_ref, half_ref,
     cols_send, rows_recv, rows_all, cols_recv, corner_recv,
     assigned, nodes_all, totals, sent, parts, degree_ref,
-    x_sem, in_sem, halo_send, halo_recv, z_send, z_recv,
+    x_sem, in_sem, halo_send, halo_recv, col_send, col_recv, z_send, z_recv, n_send, n_recv,
 ):
     tiles, channels, rows, lon = x_ref.shape
     lat = tiles * rows
@@ -104,12 +102,29 @@
     own_edges = pl.ds(pl.multiple_of(me * share, share), share)
 
     steps = (1,) if sides == 1 else (-1, 1)
-    around = [(1, 0, 0), (-1, 0, 0)] + [(0, dy, 0) for dy in steps]
-    around += [(dx, dy, 0) for dx in (1, -1) for dy in steps]
-    around += [(0, 0, k) for k in range(1, layers)]
+    bands = lax.axis_size("gx")
+    band = lax.axis_index("gx")
+
+    def inside(dx):
+        return jnp.logical_and(band + dx >= 0, band + dx < bands)
+
+    def when_inside(dx, action):
+        @pl.when(inside(dx))
+        def _():
+            action()
+
     barrier = pltpu.get_barrier_semaphore()
-    for offset in around:
+
+    def greet(offset):
         pl.semaphore_signal(barrier, inc=1, device_id=partner(*offset), device_id_type=MESH)
+
+    peers = [(0, 0, k) for k in range(1, layers)] + [(0, dy, 0) for dy in steps]
+    for offset in peers:
+        greet(offset)
+    across = [(0,)] + [(dy,) for dy in steps]
+    for dx in (1, -1):
+        when_inside(dx, lambda: [greet((dx, *dy, 0)) for dy in across])
+    greetings = len(peers) + len(across) * (2 - (band == 0).astype(jnp.int32) - (band == bands - 1).astype(jnp.int32))
     local = [
         (w1_hbm, w1_in), (w2_hbm, w2_in), (senders_hbm, senders_ref), (receivers_hbm, receivers_ref),
         (count_hbm, count_ref), (e1_hbm, e1_ref), (e2_hbm, e2_in),
@@ -126,29 +141,103 @@
     ]
     for load in loads + local:
         load.start()
-    pl.semaphore_wait(barrier, len(around))
-
+    pl.semaphore_wait(barrier, greetings)
+
+    def along(step):
+        return jnp.logical_and(me + step >= 0, me + step < layers)
+
+    def nodes_to(block, step, source):
+        at = pl.ds(pl.multiple_of(block * shard, shard), shard)
+        return pltpu.make_async_remote_copy(
+            src_ref=source, dst_ref=nodes_all.at[at, :],
+            send_sem=n_send.at[block, step + layers - 1], recv_sem=n_recv.at[block],
+            device_id={"gz": jnp.clip(me + step, 0, layers - 1)}, device_id_type=MESH,
+        )
+
+    hops = [step for far in range(1, min(REACH, layers - 1) + 1) for step in (far, -far)]
+    passed = [(far, way) for far in range(REACH + 1, layers) for way in (1, -1)]
+
+    def every_hop(action):
+        for step in hops:
+            @pl.when(along(step))
+            def _():
+                action(nodes_to(me, step, mesh_hbm))
+
+    def every_pass(action):
+        for far, way in passed:
+            block = me - REACH * way
+            step = (far - REACH) * way
+
+            @pl.when(jnp.logical_and(along(-REACH * way), along(step)))
+            def _():
+                at = pl.ds(pl.multiple_of(block * shard, shard), shard)
+                action(nodes_to(block, step, nodes_all.at[at, :]), far == REACH + 1)
+
+    def pass_nodes(copy, first):
+        if first:
+            copy.wait_recv()
+        copy.start()
+
+    def receive_nodes():
+        for far in range(1, layers):
+            for way in (1, -1):
+                early = jnp.logical_and(far == REACH, along(way)) if passed else False
+
+                @pl.when(jnp.logical_and(along(-far * way), jnp.logical_not(early)))
+                def _():
+                    nodes_to(me - far * way, way, mesh_hbm).wait_recv()
+
+    every_hop(lambda copy: copy.start())
+
+    part = share // PARTS
     spread = []
-    for k in range(1, layers):
-        peer = lax.rem(me + k, layers)
-        theirs = pl.ds(pl.multiple_of(peer * share, share), share)
-        spread.append(
-            remote(mesh_hbm, nodes_all.at[mine, :], z_send.at[1, k], z_recv.at[1, k], (0, 0, k))
-        )
-        spread.append(
-            remote(edge_hbm.at[:, theirs], assigned.at[mine, :], z_send.at[0, k], z_recv.at[0, k], (0, 0, k))
-        )
-    halo = [
+    for c in range(PARTS):
+        for k in range(1, layers):
+            peer = lax.rem(me + k, layers)
+            theirs = pl.ds(pl.multiple_of(peer * share + c * part, part), part)
+            spread.append(
+                remote(
+                    edge_hbm.at[:, theirs], assigned.at[mine, pl.ds(c * part, part)],
+                    z_send.at[c, k], z_recv.at[c, k], (0, 0, k),
+                )
+            )
+    row_halo = [
         remote(x_hbm.at[:, pl.ds(lat - HALO, HALO), :], rows_recv.at[0], halo_send.at[0], halo_recv.at[0], (1, 0, 0)),
         remote(x_hbm.at[:, pl.ds(0, HALO), :], rows_recv.at[1], halo_send.at[1], halo_recv.at[1], (-1, 0, 0)),
     ]
-    for copy in spread + halo:
+    for copy in spread[: layers - 1]:
         copy.start()
-
-    wide[...] = jnp.zeros_like(wide)
+    for copy, dx in zip(row_halo, (1, -1)):
+        when_inside(dx, copy.start)
+    corners = []
+    for i, dy in enumerate(steps):
+        slot = sides - 1 - i
+        for n, dx in enumerate((1, -1)):
+            block = cols_send.at[lat // HALO - 1 if dx > 0 else 0]
+            at = 2 + 2 * n + i
+            corners.append(
+                (n, remote(block, corner_recv.at[n, slot], halo_send.at[at], halo_recv.at[at], (dx, dy, 0)))
+            )
+
+    def fill(n):
+        rows_recv[n] = jnp.zeros(rows_recv.shape[1:], BF16)
+        corner_recv[n] = jnp.zeros(corner_recv.shape[1:], BF16)
+
+    pl.when(band == 0)(lambda: fill(0))
+    pl.when(band == bands - 1)(lambda: fill(1))
+
+    def strips(t, i):
+        blocks = pl.ds(t * (rows // HALO), rows // HALO)
+        return remote(
+            cols_send.at[blocks], cols_recv.at[sides - 1 - i, blocks],
+            col_send.at[i, t], col_recv.at[i, t], (0, steps[i], 0),
+        )
 
     def relay(source, slot, height):
         wide[slot, pl.ds(0, channels * height), :] = source.astype(F32).reshape(channels * height, lon)
+        wide[slot, pl.ds(channels * height, (padded - channels) * height), :] = jnp.zeros(
+            ((padded - channels) * height, lon), F32
+        )
 
         def row(j):
             return wide[slot, pl.ds(j, padded, stride=height), :].astype(BF16)
@@ -161,7 +250,13 @@
         pltpu.make_async_copy(
             x_hbm.at[:, pl.ds(t * rows, rows), :], x_ref.at[t], x_sem.at[t]
         ).wait()
-        row_of = relay(x_ref[t], 0, rows)
+
+        @pl.when(t > 0)
+        def _():
+            for i in range(len(steps)):
+                strips(t - 1, i).start()
+
+        relay(x_ref[t], 0, rows)
         for half in range(rows // HALO):
             beside = jnp.zeros((padded, lon), F32)
             for j in range(HALO):
@@ -174,18 +269,11 @@
         return carry
 
     lax.fori_loop(0, tiles, widen, 0)
-    for i, dy in enumerate(steps):
-        slot = sides - 1 - i
-        halo.append(
-            remote(cols_send, cols_recv.at[slot], halo_send.at[2 + i], halo_recv.at[2 + i], (0, dy, 0))
-        )
-        for n, dx in enumerate((1, -1)):
-            block = cols_send.at[lat // HALO - 1 if dx > 0 else 0]
-            at = 4 + 2 * n + i
-            halo.append(
-                remote(block, corner_recv.at[n, slot], halo_send.at[at], halo_recv.at[at], (dx, dy, 0))
-            )
-    for copy in halo[2:]:
+    for i in range(len(steps)):
+        strips(tiles - 1, i).start()
+    for n, copy in corners:
+        when_inside(1 - 2 * n, copy.start)
+    for copy in spread[layers - 1 :]:
         copy.start()
 
     for copy in local:
@@ -203,12 +291,10 @@
     tile = lax.axis_index("gx") * lax.axis_size("gy") + lax.axis_index("gy")
     slot_ids = lax.broadcasted_iota(jnp.int32, (1, slots), 1)
     near_ref[...] = jnp.where(slot_ids < count_ref[...], receivers_ref[...] - tile * nodes, -1)
-    own_row, own_column, own_halo = locate(senders_ref[:, own_edges], lat, lon, sides)
-    place_ref[0:1, :] = own_row
-    place_ref[1:2, :] = own_halo
+    block, lane = locate(senders_ref[:, own_edges], lat, lon, sides)
+    place_ref[0:1, :] = block
     place_ref[2:3, :] = near_ref[:, own_edges]
-    cmask[...] = onehot_of(own_column, 0, lon)
-    gathered[...] = jnp.zeros_like(gathered)
+    cmask[...] = onehot_of(lane, 0, lon)
     b1 = cols[:, 0:1] * 0.5
 
     def pick_rows(first, count):
@@ -219,33 +305,32 @@
             picks.append((cmask[...].reshape(lon // 16, 16, share) * here[None]).reshape(lon, share))
         return jnp.concatenate(picks, axis=0)
 
-    def gather(g, carry):
-        gathered[...] += jnp.dot(xw[g], pick_rows(g * GROUP, GROUP), preferred_element_type=F32)
-        return carry
-
-    lax.fori_loop(0, tiles * groups, gather, 0)
-
     def first_layer(g):
         half = jnp.dot(w1[...], xw[g], preferred_element_type=F32) + b1
         return half_silu(half).astype(BF16)
 
-    def embed(t, carry):
-        own_gain = cols[mine, 1:2]
-        hidden = first_layer(t * groups)
-        for group in range(groups):
+    own_gain = cols[mine, 1:2]
+
+    def embed(start, stop):
+        hidden = first_layer(start * groups)
+        for g in range(start * groups, stop * groups):
+            t, group = g // groups, g % groups
             pre = jnp.dot(w2[...], hidden, preferred_element_type=F32)
-            if group + 1 < groups:
-                hidden = first_layer(t * groups + group + 1)
+            if g + 1 < stop * groups:
+                hidden = first_layer(g + 1)
             own = pre[:shard, :] * inverse_spread(pre) * own_gain
             for r in range(GROUP):
-                out_wide[pl.ds(group * GROUP + r, shard, stride=rows), :] = own[
+                out_wide[t, pl.ds(group * GROUP + r, shard, stride=rows), :] = own[
                     :, r * lon : (r + 1) * lon
                 ]
-        stage[t] = out_wide[...].reshape(shard, rows, lon).astype(BF16)
-        return carry
-
-    lax.fori_loop(0, EARLY, embed, 0)
-
+            if group + 1 == groups:
+                stage[t] = out_wide[t].reshape(shard, rows, lon).astype(BF16)
+
+    picked = jnp.zeros((padded, share), F32)
+    for t in range(tiles):
+        cells = jnp.concatenate([xw[t * groups + g] for g in range(groups)], axis=1)
+        picked = picked + jnp.dot(cells, pick_rows(t * rows, rows), preferred_element_type=F32)
+    half_ref[0:padded, :] = picked
     last = (((1,), (1,)), ((), ()))
     degree = jnp.zeros((8, nodes), F32)
     for start in range(0, slots, share):
@@ -253,57 +338,74 @@
         ones = jnp.ones((8, share), BF16)
         degree = degree + lax.dot_general(ones, chunk, last, preferred_element_type=F32)
     degree_ref[...] = jnp.maximum(degree, 1.0)
-
-    for copy in halo:
-        copy.wait()
+    embed(0, 1)
+
+    every_pass(pass_nodes)
+    for n, copy in enumerate(row_halo):
+        when_inside(1 - 2 * n, copy.wait_send)
+        when_inside(2 * n - 1, copy.wait_recv)
     for i in range(2):
         row_of = relay(rows_recv[i], 0, HALO)
         for j in range(HALO):
             rows_all[i, :, j * lon : (j + 1) * lon] = row_of(j)
-    picked = gathered[...]
-    pieces = [rows_all[0], rows_all[1]]
-    for side in range(sides):
-        pieces.append(jnp.concatenate([cols_recv[side, b] for b in range(lat // HALO)], axis=1))
-    pieces.append(jnp.concatenate([corner_recv[n, side] for n in range(2) for side in range(sides)], axis=1))
-    first = 0
-    for piece in pieces:
-        pick = onehot_of(place_ref[1:2, :], first, piece.shape[1])
-        picked = picked + jnp.dot(piece, pick, preferred_element_type=F32)
-        first += piece.shape[1]
+    cells = jnp.concatenate([rows_all[0], rows_all[1]], axis=1)
+    half_ref[0:padded, :] += jnp.dot(cells, pick_rows(lat, 2 * HALO), preferred_element_type=F32)
+    embed(1, EARLY)
+
+    for t in range(tiles):
+        for i in range(len(steps)):
+            strips(t, i).wait()
+    for n, copy in corners:
+        when_inside(1 - 2 * n, copy.wait_send)
+        when_inside(2 * n - 1, copy.wait_recv)
+    pieces = [cols_recv[side, b] for side in range(sides) for b in range(lat // HALO)]
+    pieces += [corner_recv[n, side] for n in range(2) for side in range(sides)]
+    cells = jnp.concatenate(pieces, axis=1)
+    picked = half_ref[0:padded, :] + jnp.dot(
+        cells, pick_rows(lat + 2 * HALO, cells.shape[1] // lon), preferred_element_type=F32
+    )
     half = jnp.dot(w1[...], picked.astype(BF16), preferred_element_type=F32) + b1
     hidden = half_silu(half).astype(BF16)
     pre = jnp.dot(w2[...], hidden, preferred_element_type=F32)
     scale = inverse_spread(pre)
     for k in range(layers):
         block = pl.ds(pl.multiple_of(lax.rem(me + k, layers) * shard, shard), shard)
-        part = pre[k * shard : (k + 1) * shard, :] * scale * cols[block, 1:2]
-        sender_ref[block, :] = part.astype(BF16)
+        rows_k = pre[k * shard : (k + 1) * shard, :] * scale * cols[block, 1:2]
+        sender_ref[block, :] = rows_k.astype(BF16)
     half_ref[...] = jnp.dot(e1_ref[:, latent : 2 * latent], sender_ref[...], preferred_element_type=F32)
 
-    for copy in spread:
-        copy.wait()
+    receive_nodes()
     onehot = onehot_of(place_ref[2:3, :], 0, nodes)
     mesh_cols = jnp.dot(nodes_all[...], onehot, preferred_element_type=F32).astype(BF16)
-    half = half_ref[...] + jnp.dot(e1_ref[:, :latent], assigned[...], preferred_element_type=F32)
-    half = half + jnp.dot(e1_ref[:, 2 * latent :], mesh_cols, preferred_element_type=F32)
-    hidden = half_silu((half + cols[:, 2:3]) * 0.5).astype(BF16)
-    second = jnp.dot(e2_ref[...], hidden, preferred_element_type=F32)
-    message = (
-        assigned[...].astype(F32) + second * inverse_spread(second) * cols[:, 3:4] + cols[:, 4:5]
-    ).astype(BF16)
-    totals[...] = lax.dot_general(message, onehot, last, preferred_element_type=F32)
+    half_ref[...] += jnp.dot(e1_ref[:, 2 * latent :], mesh_cols, preferred_element_type=F32) + cols[:, 2:3]
+
+    for c in range(PARTS):
+        for copy in spread[c * (layers - 1) : (c + 1) * (layers - 1)]:
+            copy.wait()
+        at = slice(c * part, (c + 1) * part)
+        half = half_ref[:, at] + jnp.dot(e1_ref[:, :latent], assigned[:, at], preferred_element_type=F32)
+        hidden = half_silu(half * 0.5).astype(BF16)
+        second = jnp.dot(e2_ref[...], hidden, preferred_element_type=F32)
+        message = (
+            assigned[:, at].astype(F32) + second * inverse_spread(second) * cols[:, 3:4] + cols[:, 4:5]
+        ).astype(BF16)
+        onehot = onehot_of(place_ref[2:3, at], 0, nodes)
+        sums = lax.dot_general(message, onehot, last, preferred_element_type=F32)
+        totals[...] = sums if c == 0 else totals[...] + sums
     sent[...] = totals[...].astype(BF16)
+    every_hop(lambda copy: copy.wait_send())
+    every_pass(lambda copy, first: copy.wait_send())
     exchange = []
     for k in range(1, layers):
         peer = lax.rem(me + k, layers)
         theirs = pl.ds(pl.multiple_of(peer * shard, shard), shard)
         exchange.append(
-            remote(sent.at[theirs, :], parts.at[k], z_send.at[2, k], z_recv.at[2, k], (0, 0, k))
+            remote(sent.at[theirs, :], parts.at[k], z_send.at[PARTS, k], z_recv.at[PARTS, k], (0, 0, k))
         )
     for copy in exchange:
         copy.start()
 
-    lax.fori_loop(EARLY, tiles, embed, 0)
+    embed(EARLY, tiles)
 
     for copy in exchange:
         copy.wait()
@@ -377,8 +479,7 @@
         ((1, slots), I32),
         ((8, share), I32),
         ((lon, share), BF16),
-        ((padded, share), F32),
-        ((shard * ROWS, lon), F32),
+        ((tiles, shard * ROWS, lon), F32),
         ((latent, share), BF16),
         ((latent, share), F32),
         ((lat // HALO, padded, lon), BF16),
@@ -393,7 +494,7 @@
         ((layers, shard, nodes), BF16),
         ((8, nodes), F32),
     ]
-    sems = [(tiles,), (14,), (8,), (8,), (3, layers), (3, layers)]
+    sems = [(tiles,), (14,), (8,), (8,), (sides, tiles), (sides, tiles), (PARTS + 1, layers), (PARTS + 1, layers), (layers, 2 * layers - 1), (layers,)]
     line = lambda v: v.reshape(1, v.size)
     stage, mean = pl.pallas_call(
         kernel,

time: 35.7 us -> 33.5 us (0.938)
  Pallas kernels: 34.2 us -> 31.9 us
    pallas_call x1, Pallas kernels: 32.9 us -> 30.5 us  [on_device(): pl.pallas_call(kernel, in_specs=[hbm] * 15, out_specs=[vmem, vmem], out_s...]
where the time goes in v3:
time: 33.5 us; the launch traced here: 33.4 us
  Pallas kernels  31.9 us (95%)
  between operations  1.45 us (4%)
    pallas_call x1, Pallas kernels, on_device(): pl.pallas_call(kernel, in_specs=[hbm] * 15, out_specs=[vmem, vmem], out_s...  30.5 us
    pallas_call x1, Pallas kernels, on_device(): pl.pallas_call(finish, in_specs=[vmem, vmem], out_specs=[hbm, hbm], out_s...  1.37 us

profile of v3, /device:TPU:0, one launch (start us, length us, event | category | flops | bytes accessed | tf_op | source)
XLA Modules:
  0.0 33.4 jit_solution(8750769541878646202)
XLA Ops:
  1.3 30.5 %shard_map.158 = (bf16[4,128,16,128]{3,2,1,0:T(8,128)(2,1)S(1)}, bf16[128,256]{1,0:T(8,128)(2,1)S(1)}) custom-call(bf16[186,64,128]{2,1,0:T(8,128)(2,1)} %x_hbm.1, bf16[186,512]{1,0:T(8,128)(2,1)} %bitcast.12, bf16[512,512]{1,0:T(8,128)(2,1)} %w2_hbm.1, bf16[512,1536]{1,0:T(8,128)(2,1)} %e1_hbm.1, bf16[512,512]{1,0:T(8,128)(2,1)} %e2_hbm.1, ...), custom_call_target="tpu_custom_call" | custom-call | tf_op jit(solution)/shard_map/pallas_call | solution.py:499
  31.8 1.4 %shard_map.159 = (bf16[128,64,128]{2,1,0:T(8,128)(2,1)}, bf16[128,256]{1,0:T(8,128)(2,1)}) custom-call(bf16[4,128,16,128]{3,2,1,0:T(8,128)(2,1)S(1)} %get-tuple-element.6.stage, bf16[128,256]{1,0:T(8,128)(2,1)S(1)} %get-tuple-element.7.mesh_ref), custom_call_target="tpu_custom_call" | custom-call | tf_op jit(solution)/shard_map/pallas_call | solution.py:517

commit v4 on v3

--- a/solution.py
+++ b/solution.py
@@ -10,7 +10,6 @@
 GROUP = 4
 EARLY = 2
 PARTS = 2
-REACH = 2
 
 epsilon = 1e-05
 F32 = jnp.float32
@@ -141,74 +140,80 @@
     ]
     for load in loads + local:
         load.start()
-    pl.semaphore_wait(barrier, greetings)
-
-    def along(step):
-        return jnp.logical_and(me + step >= 0, me + step < layers)
-
-    def nodes_to(block, step, source):
+
+    half_layers = layers // 2
+    side = me // half_layers
+    paired = layers == 4
+    mate = me + 1 - 2 * lax.rem(me, 2)
+    far_peers = [lax.rem((1 - side) * half_layers + j, layers) for j in range(half_layers)]
+    near_peers = [side * half_layers + lax.rem(me + j, half_layers) for j in range(1, half_layers)]
+    order = far_peers + near_peers
+    if 2 * half_layers != layers:
+        order = [lax.rem(me + k, layers) for k in range(1, layers)]
+
+    def to_layer(source, target, send_sem, recv_sem, peer):
+        return pltpu.make_async_remote_copy(
+            src_ref=source, dst_ref=target, send_sem=send_sem, recv_sem=recv_sem,
+            device_id={"gz": peer}, device_id_type=MESH,
+        )
+
+    def nodes_to(block, peer, slot, source):
         at = pl.ds(pl.multiple_of(block * shard, shard), shard)
-        return pltpu.make_async_remote_copy(
-            src_ref=source, dst_ref=nodes_all.at[at, :],
-            send_sem=n_send.at[block, step + layers - 1], recv_sem=n_recv.at[block],
-            device_id={"gz": jnp.clip(me + step, 0, layers - 1)}, device_id_type=MESH,
-        )
-
-    hops = [step for far in range(1, min(REACH, layers - 1) + 1) for step in (far, -far)]
-    passed = [(far, way) for far in range(REACH + 1, layers) for way in (1, -1)]
-
-    def every_hop(action):
-        for step in hops:
-            @pl.when(along(step))
+        return to_layer(source, nodes_all.at[at, :], n_send.at[slot], n_recv.at[block], peer)
+
+    if paired:
+        direct = [nodes_to(me, peer, i, mesh_hbm) for i, peer in enumerate((2 - side, mate))]
+    else:
+        direct = [nodes_to(me, peer, i, mesh_hbm) for i, peer in enumerate(order)]
+    is_hub = jnp.logical_and(me > 0, me < layers - 1)
+
+    def passed():
+        return [
+            nodes_to(block, mate, 2 + i, nodes_all.at[pl.ds(pl.multiple_of(block * shard, shard), shard), :])
+            for i, block in enumerate(far_peers)
+        ]
+
+    def pass_nodes():
+        if paired:
+            @pl.when(is_hub)
             def _():
-                action(nodes_to(me, step, mesh_hbm))
-
-    def every_pass(action):
-        for far, way in passed:
-            block = me - REACH * way
-            step = (far - REACH) * way
-
-            @pl.when(jnp.logical_and(along(-REACH * way), along(step)))
+                for copy in passed():
+                    copy.wait_recv()
+                    copy.start()
+
+    def receive_nodes():
+        for i, block in enumerate(near_peers if paired else order):
+            nodes_to(block, mate, i, mesh_hbm).wait_recv()
+        if paired:
+            @pl.when(jnp.logical_not(is_hub))
             def _():
-                at = pl.ds(pl.multiple_of(block * shard, shard), shard)
-                action(nodes_to(block, step, nodes_all.at[at, :]), far == REACH + 1)
-
-    def pass_nodes(copy, first):
-        if first:
-            copy.wait_recv()
-        copy.start()
-
-    def receive_nodes():
-        for far in range(1, layers):
-            for way in (1, -1):
-                early = jnp.logical_and(far == REACH, along(way)) if passed else False
-
-                @pl.when(jnp.logical_and(along(-far * way), jnp.logical_not(early)))
-                def _():
-                    nodes_to(me - far * way, way, mesh_hbm).wait_recv()
-
-    every_hop(lambda copy: copy.start())
+                for copy in passed():
+                    copy.wait_recv()
+
+    def sent_nodes():
+        for copy in direct:
+            copy.wait_send()
+        if paired:
+            @pl.when(is_hub)
+            def _():
+                for copy in passed():
+                    copy.wait_send()
 
     part = share // PARTS
     spread = []
     for c in range(PARTS):
-        for k in range(1, layers):
-            peer = lax.rem(me + k, layers)
+        for k, peer in enumerate(order):
             theirs = pl.ds(pl.multiple_of(peer * share + c * part, part), part)
             spread.append(
-                remote(
+                to_layer(
                     edge_hbm.at[:, theirs], assigned.at[mine, pl.ds(c * part, part)],
-                    z_send.at[c, k], z_recv.at[c, k], (0, 0, k),
+                    z_send.at[c, k], z_recv.at[c, me], peer,
                 )
             )
     row_halo = [
         remote(x_hbm.at[:, pl.ds(lat - HALO, HALO), :], rows_recv.at[0], halo_send.at[0], halo_recv.at[0], (1, 0, 0)),
         remote(x_hbm.at[:, pl.ds(0, HALO), :], rows_recv.at[1], halo_send.at[1], halo_recv.at[1], (-1, 0, 0)),
     ]
-    for copy in spread[: layers - 1]:
-        copy.start()
-    for copy, dx in zip(row_halo, (1, -1)):
-        when_inside(dx, copy.start)
     corners = []
     for i, dy in enumerate(steps):
         slot = sides - 1 - i
@@ -233,6 +238,12 @@
             col_send.at[i, t], col_recv.at[i, t], (0, steps[i], 0),
         )
 
+    def send_strips(t):
+        for i in range(len(steps)):
+            strips(t, i).start()
+
+    ahead = jnp.maximum(tiles - 1 - me, 0)
+
     def relay(source, slot, height):
         wide[slot, pl.ds(0, channels * height), :] = source.astype(F32).reshape(channels * height, lon)
         wide[slot, pl.ds(channels * height, (padded - channels) * height), :] = jnp.zeros(
@@ -250,11 +261,6 @@
         pltpu.make_async_copy(
             x_hbm.at[:, pl.ds(t * rows, rows), :], x_ref.at[t], x_sem.at[t]
         ).wait()
-
-        @pl.when(t > 0)
-        def _():
-            for i in range(len(steps)):
-                strips(t - 1, i).start()
 
         relay(x_ref[t], 0, rows)
         for half in range(rows // HALO):
@@ -268,9 +274,28 @@
             cols_send[t * (rows // HALO) + half] = beside.astype(BF16)
         return carry
 
-    lax.fori_loop(0, tiles, widen, 0)
-    for i in range(len(steps)):
-        strips(tiles - 1, i).start()
+    lax.fori_loop(0, ahead, widen, 0)
+    pl.semaphore_wait(barrier, greetings)
+    for copy in direct + spread[: layers - 1]:
+        copy.start()
+    for copy, dx in zip(row_halo, (1, -1)):
+        when_inside(dx, copy.start)
+
+    def send_ready(t, carry):
+        send_strips(t)
+        return carry
+
+    lax.fori_loop(0, ahead, send_ready, 0)
+
+    def widen_and_send(t, carry):
+        @pl.when(t > ahead)
+        def _():
+            send_strips(t - 1)
+
+        return widen(t, carry)
+
+    lax.fori_loop(ahead, tiles, widen_and_send, 0)
+    send_strips(tiles - 1)
     for n, copy in corners:
         when_inside(1 - 2 * n, copy.start)
     for copy in spread[layers - 1 :]:
@@ -331,6 +356,7 @@
         cells = jnp.concatenate([xw[t * groups + g] for g in range(groups)], axis=1)
         picked = picked + jnp.dot(cells, pick_rows(t * rows, rows), preferred_element_type=F32)
     half_ref[0:padded, :] = picked
+    pass_nodes()
     last = (((1,), (1,)), ((), ()))
     degree = jnp.zeros((8, nodes), F32)
     for start in range(0, slots, share):
@@ -340,7 +366,6 @@
     degree_ref[...] = jnp.maximum(degree, 1.0)
     embed(0, 1)
 
-    every_pass(pass_nodes)
     for n, copy in enumerate(row_halo):
         when_inside(1 - 2 * n, copy.wait_send)
         when_inside(2 * n - 1, copy.wait_recv)
@@ -380,8 +405,12 @@
     half_ref[...] += jnp.dot(e1_ref[:, 2 * latent :], mesh_cols, preferred_element_type=F32) + cols[:, 2:3]
 
     for c in range(PARTS):
-        for copy in spread[c * (layers - 1) : (c + 1) * (layers - 1)]:
-            copy.wait()
+        for peer in order:
+            at = pl.ds(pl.multiple_of(peer * shard, shard), shard)
+            to_layer(
+                edge_hbm.at[:, pl.ds(0, part)], assigned.at[at, pl.ds(c * part, part)],
+                z_send.at[c, 0], z_recv.at[c, peer], peer,
+            ).wait_recv()
         at = slice(c * part, (c + 1) * part)
         half = half_ref[:, at] + jnp.dot(e1_ref[:, :latent], assigned[:, at], preferred_element_type=F32)
         hidden = half_silu(half * 0.5).astype(BF16)
@@ -393,25 +422,29 @@
         sums = lax.dot_general(message, onehot, last, preferred_element_type=F32)
         totals[...] = sums if c == 0 else totals[...] + sums
     sent[...] = totals[...].astype(BF16)
-    every_hop(lambda copy: copy.wait_send())
-    every_pass(lambda copy, first: copy.wait_send())
     exchange = []
-    for k in range(1, layers):
-        peer = lax.rem(me + k, layers)
+    for k, peer in enumerate(order):
         theirs = pl.ds(pl.multiple_of(peer * shard, shard), shard)
         exchange.append(
-            remote(sent.at[theirs, :], parts.at[k], z_send.at[PARTS, k], z_recv.at[PARTS, k], (0, 0, k))
+            to_layer(sent.at[theirs, :], parts.at[me], z_send.at[PARTS, k], z_recv.at[PARTS, me], peer)
         )
     for copy in exchange:
         copy.start()
+    sent_nodes()
+    for copy in spread:
+        copy.wait_send()
 
     embed(EARLY, tiles)
 
     for copy in exchange:
-        copy.wait()
+        copy.wait_send()
     total = totals[mine, :]
-    for k in range(1, layers):
-        total = total + parts[k].astype(F32)
+    for peer in order:
+        to_layer(
+            sent.at[pl.ds(0, shard), :], parts.at[peer], z_send.at[PARTS, 0], z_recv.at[PARTS, peer], peer
+        ).wait_recv()
+    for peer in order:
+        total = total + parts[peer].astype(F32)
     mean_ref[...] = (nodes_all[mine, :].astype(F32) + total / degree_ref[0:1, :]).astype(BF16)
 
 
@@ -494,7 +527,7 @@
         ((layers, shard, nodes), BF16),
         ((8, nodes), F32),
     ]
-    sems = [(tiles,), (14,), (8,), (8,), (sides, tiles), (sides, tiles), (PARTS + 1, layers), (PARTS + 1, layers), (layers, 2 * layers - 1), (layers,)]
+    sems = [(tiles,), (14,), (8,), (8,), (sides, tiles), (sides, tiles), (PARTS + 1, layers), (PARTS + 1, layers), (layers + 1,), (layers,)]
     line = lambda v: v.reshape(1, v.size)
     stage, mean = pl.pallas_call(
         kernel,

time: 33.5 us -> 32.4 us (0.967)
  Pallas kernels: 31.9 us -> 30.8 us
    pallas_call x1, Pallas kernels: 30.5 us -> 29.4 us  [on_device(): pl.pallas_call(kernel, in_specs=[hbm] * 15, out_specs=[vmem, vmem], out_s...]
where the time goes in v4:
time: 32.4 us; the launch traced here: 32.2 us
  Pallas kernels  30.8 us (95%)
  between operations  1.45 us (4%)
    pallas_call x1, Pallas kernels, on_device(): pl.pallas_call(kernel, in_specs=[hbm] * 15, out_specs=[vmem, vmem], out_s...  29.4 us
    pallas_call x1, Pallas kernels, on_device(): pl.pallas_call(finish, in_specs=[vmem, vmem], out_specs=[hbm, hbm], out_s...  1.37 us

profile of v4, /device:TPU:0, one launch (start us, length us, event | category | flops | bytes accessed | tf_op | source)
XLA Modules:
  0.0 32.2 jit_solution(4773498684332180957)
XLA Ops:
  1.3 29.4 %shard_map.158 = (bf16[4,128,16,128]{3,2,1,0:T(8,128)(2,1)S(1)}, bf16[128,256]{1,0:T(8,128)(2,1)S(1)}) custom-call(bf16[186,64,128]{2,1,0:T(8,128)(2,1)} %x_hbm.1, bf16[186,512]{1,0:T(8,128)(2,1)} %bitcast.12, bf16[512,512]{1,0:T(8,128)(2,1)} %w2_hbm.1, bf16[512,1536]{1,0:T(8,128)(2,1)} %e1_hbm.1, bf16[512,512]{1,0:T(8,128)(2,1)} %e2_hbm.1, ...), custom_call_target="tpu_custom_call" | custom-call | tf_op jit(solution)/shard_map/pallas_call | solution.py:532
  30.7 1.4 %shard_map.159 = (bf16[128,64,128]{2,1,0:T(8,128)(2,1)}, bf16[128,256]{1,0:T(8,128)(2,1)}) custom-call(bf16[4,128,16,128]{3,2,1,0:T(8,128)(2,1)S(1)} %get-tuple-element.6.stage, bf16[128,256]{1,0:T(8,128)(2,1)S(1)} %get-tuple-element.7.mesh_ref), custom_call_target="tpu_custom_call" | custom-call | tf_op jit(solution)/shard_map/pallas_call | solution.py:550

commit v5 on v4

--- a/solution.py
+++ b/solution.py
@@ -242,7 +242,7 @@
         for i in range(len(steps)):
             strips(t, i).start()
 
-    ahead = jnp.maximum(tiles - 1 - me, 0)
+    ahead = jnp.maximum(tiles - 1 - me - jnp.minimum(lax.axis_index("gy"), 1), 0)
 
     def relay(source, slot, height):
         wide[slot, pl.ds(0, channels * height), :] = source.astype(F32).reshape(channels * height, lon)

time: 32.4 us -> 32.9 us (1.015)
  Pallas kernels: 30.8 us -> 31.3 us
    pallas_call x1, Pallas kernels: 29.4 us -> 29.9 us  [on_device(): pl.pallas_call(kernel, in_specs=[hbm] * 15, out_specs=[vmem, vmem], out_s...]
where the time goes in v5:
time: 32.9 us; the launch traced here: 32.7 us
  Pallas kernels  31.3 us (95%)
  between operations  1.45 us (4%)
    pallas_call x1, Pallas kernels, on_device(): pl.pallas_call(kernel, in_specs=[hbm] * 15, out_specs=[vmem, vmem], out_s...  29.9 us
    pallas_call x1, Pallas kernels, on_device(): pl.pallas_call(finish, in_specs=[vmem, vmem], out_specs=[hbm, hbm], out_s...  1.37 us

profile of v5, /device:TPU:0, one launch (start us, length us, event | category | flops | bytes accessed | tf_op | source)
XLA Modules:
  0.0 32.7 jit_solution(6949824072836731145)
XLA Ops:
  1.3 29.9 %shard_map.158 = (bf16[4,128,16,128]{3,2,1,0:T(8,128)(2,1)S(1)}, bf16[128,256]{1,0:T(8,128)(2,1)S(1)}) custom-call(bf16[186,64,128]{2,1,0:T(8,128)(2,1)} %x_hbm.1, bf16[186,512]{1,0:T(8,128)(2,1)} %bitcast.12, bf16[512,512]{1,0:T(8,128)(2,1)} %w2_hbm.1, bf16[512,1536]{1,0:T(8,128)(2,1)} %e1_hbm.1, bf16[512,512]{1,0:T(8,128)(2,1)} %e2_hbm.1, ...), custom_call_target="tpu_custom_call" | custom-call | tf_op jit(solution)/shard_map/pallas_call | solution.py:532
  31.2 1.4 %shard_map.159 = (bf16[128,64,128]{2,1,0:T(8,128)(2,1)}, bf16[128,256]{1,0:T(8,128)(2,1)}) custom-call(bf16[4,128,16,128]{3,2,1,0:T(8,128)(2,1)S(1)} %get-tuple-element.6.stage, bf16[128,256]{1,0:T(8,128)(2,1)S(1)} %get-tuple-element.7.mesh_ref), custom_call_target="tpu_custom_call" | custom-call | tf_op jit(solution)/shard_map/pallas_call | solution.py:550
